TPU v7x, 32 devices: a whole 2x2x4 slice. The times are simulated.
32 devices in a mesh: grp: 2 (over x), tm: 16 (over z, y, core).
Axes of the slice: x: 2, y: 2, z: 4, core: 2. Of those that a mesh axis runs over, the one named last changes fastest.
Arguments:
- video_features: bfloat16 [32, 24, 8, 256], P('tm', 'grp'), parts along dimension 1, may hold values from -6 to 6
- cotangent: bfloat16 [32, 24, 8, 256], P('tm', 'grp'), parts along dimension 1, may hold values from -6 to 6
- encoder_weight: bfloat16 [6912, 256], replicated, may hold values from -0.078125 to 0.078125
- down_weight: bfloat16 [2048, 256], replicated, may hold values from -0.125 to 0.125
- coarse_weight: bfloat16 [768, 256], replicated, may hold values from -0.21875 to 0.21875
- up_weight: bfloat16 [256, 2048], replicated, may hold values from -0.375 to 0.375
- decoder_weight: bfloat16 [6912, 256], replicated, may hold values from -0.078125 to 0.078125
- levels: int32 [256], replicated, may hold values from 3 to 8
Outputs:
- video_grad: bfloat16 [32, 24, 8, 256], P('tm', 'grp'), parts along dimension 1
- latent_codes: bfloat16 [16, 12, 4, 256], P('tm', 'grp'), parts along dimension 1
- down_grad: float32 [4096, 256], P(('grp', 'tm')), parts along dimension 0
- coarse_grad: float32 [1536, 256], P(('grp', 'tm')), parts along dimension 0
- up_grad: float32 [512, 2048], P(('grp', 'tm')), parts along dimension 0
There are 2 independent parts, one for each index of `grp`. A program takes and returns all parts, laid end to end along the dimension named above; an argument that names none is the same for every part. Nothing has to cross between parts.
All inputs are finite; a program needn't handle non-finite values.
Results may differ from a plain program's by a relative error of at most 0.018.
The roundings to bfloat16 on the way count: a program that leaves them out, or rounds other values in their place, can miss the bound.
Values may be sent and summed in bfloat16 or wider, within the bound.
A program may use at most 64 MiB of HBM per device.

v0:
```python
import math

import jax
import jax.numpy as jnp
from jax import lax
from jax.sharding import PartitionSpec as P

two_pi = 2.0 * math.pi


def from_behind(value, axis, steps):
    count = lax.axis_size(axis)
    leading, last = (max(0, -steps), min(count, count - steps))
    return lax.ppermute(value, axis, [(source, source + steps) for source in range(leading, last)])


def tap_rows(padded, frames, tile_rows, tile_cols):
    pieces = [
        padded[step_t : step_t + frames, step_r : step_r + tile_rows, step_c : step_c + tile_cols]
        for step_t in range(3)
        for step_r in range(3)
        for step_c in range(3)
    ]
    return jnp.concatenate(pieces, axis=-1).reshape(frames * tile_rows * tile_cols, -1)


def flip_taps(weight, count):
    channels = weight.shape[1]
    blocks = weight.reshape(count, channels, channels)[::-1]
    return jnp.transpose(blocks, (0, 2, 1)).reshape(count * channels, channels)


def to_depth(field):
    frames, tile_rows, tile_cols, channels = field.shape
    split = field.reshape(frames // 2, 2, tile_rows // 2, 2, tile_cols // 2, 2, channels)
    return jnp.transpose(split, (0, 2, 4, 1, 3, 5, 6)).reshape(
        frames // 2, tile_rows // 2, tile_cols // 2, 8 * channels
    )


def from_depth(field):
    frames, tile_rows, tile_cols, packed = field.shape
    channels = packed // 8
    split = field.reshape(frames, tile_rows, tile_cols, 2, 2, 2, channels)
    return jnp.transpose(split, (0, 3, 1, 4, 2, 5, 6)).reshape(
        2 * frames, 2 * tile_rows, 2 * tile_cols, channels
    )


def transposed_product(left, right):
    return lax.dot_general(
        left, right, (((0,), (0,)), ((), ())), preferred_element_type=jnp.float32
    )


def product_with_transpose(left, right):
    return lax.dot_general(
        left, right, (((1,), (1,)), ((), ())), preferred_element_type=jnp.float32
    )


def time_columns(padded, frames):
    channels = padded.shape[-1]
    pieces = [padded[step_t : step_t + frames] for step_t in range(3)]
    return jnp.concatenate(pieces, axis=-1).reshape(-1, 3 * channels)


def spatial_pad(field):
    return jnp.pad(field, ((0, 0), (1, 1), (1, 1), (0, 0)))


def fine_patches(field):
    frames, tile_rows, tile_cols, channels = field.shape
    earlier = from_behind(field, "tm", 1)
    joined = jnp.concatenate([earlier, field], axis=0)
    return tap_rows(spatial_pad(joined), frames, tile_rows, tile_cols)


def fine_future(grad_field, weight):
    frames, tile_rows, tile_cols, channels = grad_field.shape
    later_frames = from_behind(grad_field, "tm", -1)
    joined = jnp.concatenate([grad_field, later_frames], axis=0)
    patches = tap_rows(spatial_pad(joined), frames, tile_rows, tile_cols)
    return jnp.dot(patches, flip_taps(weight, 27), preferred_element_type=jnp.float32).reshape(
        grad_field.shape
    )


def quantize(padded, frames, coarse_weight, half_range):
    columns = time_columns(padded, frames)
    pre_code = jnp.dot(columns, coarse_weight, preferred_element_type=jnp.float32)
    squashed = jnp.tanh(pre_code)
    bounded = half_range * squashed
    code_values = ((bounded - jnp.sin(two_pi * bounded) / two_pi) / half_range).astype(jnp.bfloat16)
    return (code_values, (columns, squashed, bounded))


def code_backward(code_grad, state):
    columns, squashed, bounded = state
    factor = (1.0 - jnp.cos(two_pi * bounded)) * (1.0 - squashed * squashed)
    return (code_grad.astype(jnp.float32) * factor).astype(jnp.bfloat16)


def coarse_earlier(latent):
    frames = latent.shape[0]
    shift_count = (frames + 1) // frames
    pieces = [from_behind(latent, "tm", lag_dev) for lag_dev in range(shift_count, 0, -1)]
    joined = jnp.concatenate(pieces + [latent], axis=0)
    return joined


def coarse_later(field):
    frames = field.shape[0]
    shift_count = (frames + 1) // frames
    pieces = [from_behind(field, "tm", -lag_dev) for lag_dev in range(1, shift_count + 1)]
    joined = jnp.concatenate([field] + pieces, axis=0)
    return joined


def spread_forward(latent, coarse_weight, half_range):
    code_values, state = quantize(
        coarse_earlier(latent), latent.shape[0], coarse_weight, half_range
    )
    return (code_values.reshape(latent.shape), state)


def spread_backward(code_field, state, coarse_weight):
    frames = code_field.shape[0]
    channels = code_field.shape[-1]
    pre_grad = code_backward(code_field.reshape(-1, channels), state)
    later_cols = time_columns(coarse_later(pre_grad.reshape(code_field.shape)), frames)
    latent_grad = jnp.dot(
        later_cols, flip_taps(coarse_weight, 3), preferred_element_type=jnp.float32
    ).astype(jnp.bfloat16)
    weight_term = transposed_product(state[0], pre_grad)
    return (latent_grad.reshape(code_field.shape), weight_term)


def shards(
    video_features,
    cotangent,
    encoder_weight,
    down_weight,
    coarse_weight,
    up_weight,
    decoder_weight,
    levels,
):
    frames, tile_rows, tile_cols, channels = video_features.shape
    grad_scale = 1.0 / math.sqrt(frames * lax.axis_size("tm") * tile_rows * tile_cols)
    half_range = (levels.astype(jnp.float32) - 1.0) * 0.5
    enc_patches = fine_patches(video_features)
    pre_enc = jnp.dot(enc_patches, encoder_weight, preferred_element_type=jnp.float32).reshape(
        video_features.shape
    )
    hidden = (video_features.astype(jnp.float32) + jax.nn.silu(pre_enc)).astype(jnp.bfloat16)
    stacked = to_depth(hidden)
    packed_shape = stacked.shape
    coarse_shape = packed_shape[:3] + (channels,)
    stacked_rows = stacked.reshape(-1, 8 * channels)
    latent = (
        jnp.dot(stacked_rows, down_weight, preferred_element_type=jnp.float32)
        .astype(jnp.bfloat16)
        .reshape(coarse_shape)
    )
    latent_codes, coarse_state = spread_forward(latent, coarse_weight, half_range)
    code_rows = latent_codes.reshape(-1, channels)
    back_dec = fine_future(cotangent, decoder_weight)
    decoded_grad = (cotangent.astype(jnp.float32) + back_dec).astype(jnp.bfloat16)
    depth_grad = to_depth(decoded_grad).reshape(-1, 8 * channels)
    code_grad = product_with_transpose(depth_grad, up_weight).astype(jnp.bfloat16)
    up_term = transposed_product(code_rows, depth_grad) * grad_scale
    code_field = code_grad.reshape(coarse_shape)
    latent_grad, coarse_term = spread_backward(code_field, coarse_state, coarse_weight)
    latent_rows = latent_grad.reshape(-1, channels)
    hidden_grad = from_depth(product_with_transpose(latent_rows, down_weight).reshape(packed_shape))
    down_term = transposed_product(stacked_rows, latent_rows) * grad_scale
    sigmoid_pre = jax.nn.sigmoid(pre_enc)
    enc_pre_grad = (hidden_grad * sigmoid_pre * (1.0 + pre_enc * (1.0 - sigmoid_pre))).astype(
        jnp.bfloat16
    )
    back_enc = fine_future(enc_pre_grad, encoder_weight)
    video_grad = (hidden_grad + back_enc).astype(jnp.bfloat16)
    coarse_scaled = coarse_term * grad_scale
    down_grad, coarse_grad, up_grad = (
        lax.psum_scatter(down_term, "tm", scatter_dimension=0, tiled=True),
        lax.psum_scatter(coarse_scaled, "tm", scatter_dimension=0, tiled=True),
        lax.psum_scatter(up_term, "tm", scatter_dimension=0, tiled=True),
    )
    return (video_grad, latent_codes, down_grad, coarse_grad, up_grad)


def solution(mesh):
    placed = (P("tm", "grp", None, None), P("tm", "grp", None, None), P(), P(), P(), P(), P(), P())
    return jax.shard_map(
        shards,
        mesh=mesh,
        in_specs=placed,
        out_specs=(
            P("tm", "grp", None, None),
            P("tm", "grp", None, None),
            P(("grp", "tm"), None),
            P(("grp", "tm"), None),
            P(("grp", "tm"), None),
        ),
        check_vma=False,
    )
```

profile of v0, /device:TPU:0, one launch (start us, length us, event | category | flops | bytes accessed | tf_op | source)
XLA Modules:
  0.0 232.4 jit_solution(18077929066680899294)
XLA Ops:
  7.2 0.0 copy-start
  7.2 0.0 reduce-scatter.6.cloned.1.call-start
  7.2 1.4 collective-permute-start
  8.7 3.0 %collective-permute-start.1 = (bf16[2,12,8,256]{3,2,1,0:T(8,128)(2,1)}, bf16[2,12,8,256]{3,2,1,0:T(8,128)(2,1)S(1)}, u32[]{:S(2)}, u32[]{:S(2)}) collective-permute-start(bf16[2,12,8,256]{3,2,1,0:T(8,128)(2,1)} %param.8), channel_id=1, source_target_pairs={{0,1},{1,2},{2,3},{3,4},{4,5},{5,6},{6,7},{7,8},{8,9},{9,10},{10,1... | collective-permute-start | bytes 294920 | tf_op jit(solution)/shard_map/ppermute | solution.py:14
  11.7 4.1 %reverse_bitcast_fusion.1 = bf16[27,256,256]{1,2,0:T(8,128)(2,1)} fusion(bf16[27,256,256]{2,1,0:T(8,128)(2,1)} %bitcast.59), kind=kLoop, calls=%fused_computation.3 | loop fusion | bytes 7077888 | tf_op jit(solution)/shard_map/transpose | solution.py:30
  15.9 5.8 %copy.21 = bf16[27,256,256]{2,1,0:T(8,128)(2,1)} copy(bf16[27,256,256]{1,2,0:T(8,128)(2,1)} %reverse_bitcast_fusion.1) | data formatting | bytes 7077888 | tf_op jit(solution)/shard_map/transpose | solution.py:30
  21.7 0.0 collective-permute-done.1
  21.9 0.0 copy-start.2
  22.5 1.5 copy-done.2
  23.9 0.9 add_convert_fusion
  24.9 0.1 copy.34
  25.0 0.3 convolution_convert_fusion
  25.3 4.5 %collective-permute-start.3 = (bf16[1,6,4,256]{3,2,1,0:T(4,128)(2,1)S(1)}, bf16[1,6,4,256]{3,2,1,0:T(4,128)(2,1)S(1)}, u32[]{:S(2)}, u32[]{:S(2)}) collective-permute-start(bf16[1,6,4,256]{3,2,1,0:T(4,128)(2,1)S(1)} %reshape.73), channel_id=1, source_target_pairs={{0,1},{1,2},{2,3},{3,4},{4,5},{5,6},{6,7},{7,8},{8,9},{9,10},{10,1... | collective-permute-start | bytes 36872 | tf_op jit(solution)/shard_map/ppermute | solution.py:14
  29.8 4.3 %collective-permute-start.2 = (bf16[1,6,4,256]{3,2,1,0:T(4,128)(2,1)S(1)}, bf16[1,6,4,256]{3,2,1,0:T(4,128)(2,1)S(1)}, u32[]{:S(2)}, u32[]{:S(2)}) collective-permute-start(bf16[1,6,4,256]{3,2,1,0:T(4,128)(2,1)S(1)} %reshape.73), channel_id=1, source_target_pairs={{0,2},{1,3},{2,4},{3,5},{4,6},{5,7},{6,8},{7,9},{8,10},{9,11},{10,... | collective-permute-start | bytes 36872 | tf_op jit(solution)/shard_map/ppermute | solution.py:14
  34.9 1.5 copy-done.3
  36.3 0.9 fusion.2
  37.3 0.1 copy.35
  37.4 0.0 collective-permute-done.3
  37.4 0.3 divide_convert_fusion
  37.8 0.4 fusion.6
  38.2 1.2 convolution_multiply_fusion.2
  39.3 0.0 reduce-scatter.6.cloned.1.call-update
  39.4 0.0 reduce-scatter.8.cloned.1.call-start
  39.4 1.9 convolution_multiply_fusion
  41.3 0.0 reduce-scatter.8.cloned.1.call-update
  41.3 0.0 reduce-scatter.4.cloned.1.call-start
  41.3 4.2 %reverse_bitcast_fusion = bf16[27,256,256]{1,2,0:T(8,128)(2,1)} fusion(bf16[27,256,256]{2,1,0:T(8,128)(2,1)} %bitcast.60), kind=kLoop, calls=%fused_computation.2 | loop fusion | bytes 7077888 | tf_op jit(solution)/shard_map/transpose | solution.py:30
  45.5 1.3 collective-permute-start.5
  46.8 1.3 collective-permute-start.4
  48.2 0.2 copy.24
  48.3 5.8 %copy.26 = bf16[27,256,256]{2,1,0:T(8,128)(2,1)} copy(bf16[27,256,256]{1,2,0:T(8,128)(2,1)} %reverse_bitcast_fusion) | data formatting | bytes 7077888 | tf_op jit(solution)/shard_map/transpose | solution.py:30
  54.1 0.6 reshape.80
  54.7 0.0 collective-permute-done.5
  54.7 0.0 collective-permute-done.4
  54.8 0.1 convolution_convert_fusion.2
  54.9 0.4 fusion.16
  55.3 0.2 reshape_reshape.11
  55.6 0.1 reshape.77
  55.7 0.1 multiply_convert_fusion
  55.8 1.3 collective-permute-start.6
  57.1 1.8 convolution_multiply_fusion.1
  58.9 0.0 reduce-scatter.4.cloned.1.call-update
  58.9 0.7 collective-permute-done.6
  60.4 1.5 copy-done.1
  61.9 1.5 fusion.3
  63.4 32.3 %reduce-scatter.6.cloned.1.call-done = f32[48,256]{1,0:T(8,128)} async-done(((f32[768,256]{1,0:T(8,128)}), f32[48,256]{1,0:T(8,128)}) %reduce-scatter.6.cloned.1.call-update) | async-done | bytes 49168 | tf_op jit(solution)/shard_map/reduce_scatter | solution.py:187
  95.7 65.1 %reduce-scatter.8.cloned.1.call-done = f32[16,2048]{1,0:T(8,128)} async-done(((f32[256,2048]{1,0:T(8,128)}), f32[16,2048]{1,0:T(8,128)}) %reduce-scatter.8.cloned.1.call-update) | async-done | bytes 131088 | tf_op jit(solution)/shard_map/reduce_scatter | solution.py:188
  160.8 65.1 %reduce-scatter.4.cloned.1.call-done = f32[128,256]{1,0:T(8,128)} async-done(((f32[2048,256]{1,0:T(8,128)}), f32[128,256]{1,0:T(8,128)}) %reduce-scatter.4.cloned.1.call-update) | async-done | bytes 131088 | tf_op jit(solution)/shard_map/reduce_scatter | solution.py:186
  (114 shorter events, 2.1 us)
Async XLA Ops:
  7.2 17.9 %copy-start = (bf16[2048,256]{1,0:T(8,128)(2,1)S(1)}, bf16[2048,256]{1,0:T(8,128)(2,1)}, u32[]{:S(2)}) copy-start(bf16[2048,256]{1,0:T(8,128)(2,1)} %param.11) | copy-start | bytes 3145732
  7.2 88.5 %reduce-scatter.6.cloned.1.call-start = ((), (), s32[]{:S(2)}) async-start(), calls=%async_computation.4 | async-start | bytes 835584 | tf_op jit(solution)/shard_map/reduce_scatter | solution.py:187
  7.2 26.9 %collective-permute-start = (bf16[2,12,8,256]{3,2,1,0:T(8,128)(2,1)}, bf16[2,12,8,256]{3,2,1,0:T(8,128)(2,1)S(1)}, u32[]{:S(2)}, u32[]{:S(2)}) collective-permute-start(bf16[2,12,8,256]{3,2,1,0:T(8,128)(2,1)} %param.9), channel_id=1, source_target_pairs={{1,0},{2,1},{3,2},{4,3},{5,4},{6,5},{7,6},{8,7},{9,8},{10,9},{11,1... | collective-permute-start | bytes 294920 | tf_op jit(solution)/shard_map/ppermute | solution.py:14
  8.7 13.0 %collective-permute-start.1 = (bf16[2,12,8,256]{3,2,1,0:T(8,128)(2,1)}, bf16[2,12,8,256]{3,2,1,0:T(8,128)(2,1)S(1)}, u32[]{:S(2)}, u32[]{:S(2)}) collective-permute-start(bf16[2,12,8,256]{3,2,1,0:T(8,128)(2,1)} %param.8), channel_id=1, source_target_pairs={{0,1},{1,2},{2,3},{3,4},{4,5},{5,6},{6,7},{7,8},{8,9},{9,10},{10,1... | collective-permute-start | bytes 294920 | tf_op jit(solution)/shard_map/ppermute | solution.py:14
  15.9 5.8 %copy-start.8 = (s32[256]{0:T(256)S(1)}, s32[256]{0:T(256)}, u32[]{:S(2)}) copy-start(s32[256]{0:T(256)} %param.15) | copy-start | bytes 3076
  15.9 5.8 %copy-start.7 = (bf16[2,12,8,256]{3,2,1,0:T(8,128)(2,1)S(1)}, bf16[2,12,8,256]{3,2,1,0:T(8,128)(2,1)}, u32[]{:S(2)}) copy-start(bf16[2,12,8,256]{3,2,1,0:T(8,128)(2,1)} %param.9) | copy-start | bytes 294916
  15.9 5.8 %copy-start.6 = (bf16[2,12,8,256]{3,2,1,0:T(8,128)(2,1)S(1)}, bf16[2,12,8,256]{3,2,1,0:T(8,128)(2,1)}, u32[]{:S(2)}) copy-start(bf16[2,12,8,256]{3,2,1,0:T(8,128)(2,1)} %param.8) | copy-start | bytes 294916
  21.9 2.0 copy-start.2
  25.3 12.1 %collective-permute-start.3 = (bf16[1,6,4,256]{3,2,1,0:T(4,128)(2,1)S(1)}, bf16[1,6,4,256]{3,2,1,0:T(4,128)(2,1)S(1)}, u32[]{:S(2)}, u32[]{:S(2)}) collective-permute-start(bf16[1,6,4,256]{3,2,1,0:T(4,128)(2,1)S(1)} %reshape.73), channel_id=1, source_target_pairs={{0,1},{1,2},{2,3},{3,4},{4,5},{5,6},{6,7},{7,8},{8,9},{9,10},{10,1... | collective-permute-start | bytes 36872 | tf_op jit(solution)/shard_map/ppermute | solution.py:14
  29.8 7.6 %collective-permute-start.2 = (bf16[1,6,4,256]{3,2,1,0:T(4,128)(2,1)S(1)}, bf16[1,6,4,256]{3,2,1,0:T(4,128)(2,1)S(1)}, u32[]{:S(2)}, u32[]{:S(2)}) collective-permute-start(bf16[1,6,4,256]{3,2,1,0:T(4,128)(2,1)S(1)} %reshape.73), channel_id=1, source_target_pairs={{0,2},{1,3},{2,4},{3,5},{4,6},{5,7},{6,8},{7,9},{8,10},{9,11},{10,... | collective-permute-start | bytes 36872 | tf_op jit(solution)/shard_map/ppermute | solution.py:14
  34.3 2.0 copy-start.3
  36.3 1.1 copy-start.4
  36.3 1.4 copy-start.5
  39.4 121.4 %reduce-scatter.8.cloned.1.call-start = ((), (), s32[]{:S(2)}) async-start(), calls=%async_computation.5 | async-start | bytes 2228224 | tf_op jit(solution)/shard_map/reduce_scatter | solution.py:188
  41.3 184.6 %reduce-scatter.4.cloned.1.call-start = ((), (), s32[]{:S(2)}) async-start(), calls=%async_computation.3 | async-start | bytes 2228224 | tf_op jit(solution)/shard_map/reduce_scatter | solution.py:186
  45.5 9.2 %collective-permute-start.5 = (bf16[1,6,4,256]{3,2,1,0:T(4,128)(2,1)S(1)}, bf16[1,6,4,256]{3,2,1,0:T(4,128)(2,1)S(1)}, u32[]{:S(2)}, u32[]{:S(2)}) collective-permute-start(bf16[1,6,4,256]{3,2,1,0:T(4,128)(2,1)S(1)} %reshape.74), channel_id=1, source_target_pairs={{2,0},{3,1},{4,2},{5,3},{6,4},{7,5},{8,6},{9,7},{10,8},{11,9},{12,... | collective-permute-start | bytes 36872 | tf_op jit(solution)/shard_map/ppermute | solution.py:14
  46.8 7.9 %collective-permute-start.4 = (bf16[1,6,4,256]{3,2,1,0:T(4,128)(2,1)S(1)}, bf16[1,6,4,256]{3,2,1,0:T(4,128)(2,1)S(1)}, u32[]{:S(2)}, u32[]{:S(2)}) collective-permute-start(bf16[1,6,4,256]{3,2,1,0:T(4,128)(2,1)S(1)} %reshape.74), channel_id=1, source_target_pairs={{1,0},{2,1},{3,2},{4,3},{5,4},{6,5},{7,6},{8,7},{9,8},{10,9},{11,1... | collective-permute-start | bytes 36872 | tf_op jit(solution)/shard_map/ppermute | solution.py:14
  55.8 3.8 %collective-permute-start.6 = (bf16[2,12,8,256]{3,2,1,0:T(8,128)(2,1)S(1)}, bf16[2,12,8,256]{3,2,1,0:T(8,128)(2,1)S(1)}, u32[]{:S(2)}, u32[]{:S(2)}) collective-permute-start(bf16[2,12,8,256]{3,2,1,0:T(8,128)(2,1)S(1)} %multiply_convert_fusion), channel_id=1, source_target_pairs={{1,0},{2,1},{3,2},{4,3},{5,4},{6,5},{7,6},{8,7},{9,8},{10,9},{11,1... | collective-permute-start | bytes 294920 | tf_op jit(solution)/shard_map/ppermute | solution.py:14
  59.9 2.0 copy-start.1
Sparse Core Ops, SparseCore 0:
  39.5 56.1 reduce-scatter.5
  100.0 60.7 reduce-scatter.7
  165.1 60.6 reduce-scatter.3
where the time goes:
time: 233 us; the launch traced here: 232 us
  waiting for transfers between devices  163 us (70%)
  local copies, waits for them, and re-layouts  27.6 us (12%)
  starting transfers between devices  17.2 us (7%)
  between operations  14.7 us (6%)
  matrix products  9.6 us (4%)
    reduce_scatter x1, waiting for transfers between devices, shards(): lax.psum_scatter(up_term, 'tm', scatter_dimension=0, tiled=True)  65.1 us
    reduce_scatter x1, waiting for transfers between devices, shards(): lax.psum_scatter(down_term, 'tm', scatter_dimension=0, tiled=True)  65.1 us
    reduce_scatter x1, waiting for transfers between devices, shards(): lax.psum_scatter(coarse_scaled, 'tm', scatter_dimension=0, tiled=True)  32.3 us
    transpose x6, local copies, waits for them, and re-layouts, flip_taps(): return jnp.transpose(blocks, (0, 2, 1)).reshape(count * channels, channels)  20.1 us
    ppermute x7, starting transfers between devices, from_behind(): lax.ppermute(value, axis, [(source, source + steps) for source in range(l...  17.1 us
    unnamed x97, local copies, waits for them, and re-layouts  6.02 us
    dot_general x3, matrix products, transposed_product(): lax.dot_general(left, right, (((0,), (0,)), ((), ())), preferred_element_...  4.85 us
  transfers between devices with their start and end apart: 10, of which 4 were waited for; matrix products, arithmetic and copies ran while one was open for 13% of the time, Pallas kernels for 0%

commit v1 on v0

--- a/solution.py
+++ b/solution.py
@@ -132,8 +132,7 @@
     latent_grad = jnp.dot(
         later_cols, flip_taps(coarse_weight, 3), preferred_element_type=jnp.float32
     ).astype(jnp.bfloat16)
-    weight_term = transposed_product(state[0], pre_grad)
-    return (latent_grad.reshape(code_field.shape), weight_term)
+    return (latent_grad.reshape(code_field.shape), pre_grad)
 
 
 def shards(
@@ -169,24 +168,36 @@
     decoded_grad = (cotangent.astype(jnp.float32) + back_dec).astype(jnp.bfloat16)
     depth_grad = to_depth(decoded_grad).reshape(-1, 8 * channels)
     code_grad = product_with_transpose(depth_grad, up_weight).astype(jnp.bfloat16)
-    up_term = transposed_product(code_rows, depth_grad) * grad_scale
     code_field = code_grad.reshape(coarse_shape)
-    latent_grad, coarse_term = spread_backward(code_field, coarse_state, coarse_weight)
+    latent_grad, pre_grad = spread_backward(code_field, coarse_state, coarse_weight)
     latent_rows = latent_grad.reshape(-1, channels)
     hidden_grad = from_depth(product_with_transpose(latent_rows, down_weight).reshape(packed_shape))
-    down_term = transposed_product(stacked_rows, latent_rows) * grad_scale
     sigmoid_pre = jax.nn.sigmoid(pre_enc)
     enc_pre_grad = (hidden_grad * sigmoid_pre * (1.0 + pre_enc * (1.0 - sigmoid_pre))).astype(
         jnp.bfloat16
     )
     back_enc = fine_future(enc_pre_grad, encoder_weight)
     video_grad = (hidden_grad + back_enc).astype(jnp.bfloat16)
-    coarse_scaled = coarse_term * grad_scale
-    down_grad, coarse_grad, up_grad = (
-        lax.psum_scatter(down_term, "tm", scatter_dimension=0, tiled=True),
-        lax.psum_scatter(coarse_scaled, "tm", scatter_dimension=0, tiled=True),
-        lax.psum_scatter(up_term, "tm", scatter_dimension=0, tiled=True),
-    )
+    count = lax.axis_size("tm")
+
+    def slices(rows):
+        return rows.reshape(rows.shape[0], count, -1).transpose(1, 0, 2)
+
+    left = jnp.concatenate(
+        [slices(stacked_rows), slices(coarse_state[0]), slices(code_rows)], axis=-1
+    )
+    left = lax.all_to_all(left, "tm", 0, 0, tiled=True)
+    left = left.reshape(-1, left.shape[-1])
+    right = lax.all_gather(jnp.concatenate([latent_rows, pre_grad], axis=-1), "tm", tiled=True)
+    depth_all = lax.all_gather(depth_grad, "tm", tiled=True)
+    down_cols = stacked_rows.shape[1] // count
+    coarse_cols = coarse_state[0].shape[1] // count
+    down_grad = transposed_product(left[:, :down_cols], right[:, :channels]) * grad_scale
+    coarse_grad = (
+        transposed_product(left[:, down_cols : down_cols + coarse_cols], right[:, channels:])
+        * grad_scale
+    )
+    up_grad = transposed_product(left[:, down_cols + coarse_cols :], depth_all) * grad_scale
     return (video_grad, latent_codes, down_grad, coarse_grad, up_grad)
 
 

time: 233 us -> 105 us (0.45)
  waiting for transfers between devices: 163 us -> 0.04 us
  blocking collectives: 0 us -> 24.2 us
  starting transfers between devices: 17.2 us -> 24.9 us
  local copies, waits for them, and re-layouts: 27.6 us -> 30.3 us
    reduce_scatter x3 -> x0, waiting for transfers between devices: 162 us -> none  [the longest x1 65.1 us: shards(): lax.psum_scatter(up_term, 'tm', scatter_dimension=0, tiled=True)]
    all_gather x0 -> x1, blocking collectives: none -> 24.2 us  [shards(): lax.all_gather(jnp.concatenate([latent_rows, pre_grad], axis=-1), 'tm', t...]
    all_to_all x0 -> x1, starting transfers between devices: none -> 7.79 us  [shards(): left = lax.all_to_all(left, 'tm', 0, 0, tiled=True)]
  transfers between devices with their start and end apart: 10 -> 9, of which waited for: 4 -> 0; matrix products, arithmetic and copies ran while one was open for 13% -> 32% of each run, Pallas kernels for 0% -> 0%
where the time goes in v1:
time: 105 us
  local copies, waits for them, and re-layouts  30.3 us (29%)
  starting transfers between devices  24.9 us (24%)
  blocking collectives  24.2 us (23%)
  between operations  15 us (14%)
  matrix products  9.81 us (9%)
    all_gather x1, blocking collectives, shards(): lax.all_gather(jnp.concatenate([latent_rows, pre_grad], axis=-1), 'tm', t...  24.2 us
    transpose x6, local copies, waits for them, and re-layouts, flip_taps(): return jnp.transpose(blocks, (0, 2, 1)).reshape(count * channels, channels)  21.1 us
    ppermute x7, starting transfers between devices, from_behind(): lax.ppermute(value, axis, [(source, source + steps) for source in range(l...  17.1 us
    all_to_all x1, starting transfers between devices, shards(): left = lax.all_to_all(left, 'tm', 0, 0, tiled=True)  7.79 us
    unnamed x97, local copies, waits for them, and re-layouts  6.02 us
    dot_general x3, matrix products, transposed_product(): lax.dot_general(left, right, (((0,), (0,)), ((), ())), preferred_element_...  4.18 us
    dot_general x2, matrix products, fine_future(): jnp.dot(patches, flip_taps(weight, 27), preferred_element_type=jnp.float32)  2.35 us
  transfers between devices with their start and end apart: 9, of which 0 were waited for; matrix products, arithmetic and copies ran while one was open for 32% of the time, Pallas kernels for 0%

profile of v1, /device:TPU:0, one launch (start us, length us, event | category | flops | bytes accessed | tf_op | source)
XLA Modules:
  0.0 104.6 jit_solution(12740343813124322159)
XLA Ops:
  7.2 0.0 copy-start
  7.2 0.0 all-gather.2.cloned.1.call-start
  7.2 1.4 %collective-permute-start = (bf16[2,12,8,256]{3,2,1,0:T(8,128)(2,1)}, bf16[2,12,8,256]{3,2,1,0:T(8,128)(2,1)S(1)}, u32[]{:S(2)}, u32[]{:S(2)}) collective-permute-start(bf16[2,12,8,256]{3,2,1,0:T(8,128)(2,1)} %param.9), channel_id=1, source_target_pairs={{1,0},{2,1},{3,2},{4,3},{5,4},{6,5},{7,6},{8,7},{9,8},{10,9},{11,1... | collective-permute-start | bytes 294920 | tf_op jit(solution)/shard_map/ppermute | solution.py:14
  8.7 3.0 %collective-permute-start.1 = (bf16[2,12,8,256]{3,2,1,0:T(8,128)(2,1)}, bf16[2,12,8,256]{3,2,1,0:T(8,128)(2,1)S(1)}, u32[]{:S(2)}, u32[]{:S(2)}) collective-permute-start(bf16[2,12,8,256]{3,2,1,0:T(8,128)(2,1)} %param.8), channel_id=1, source_target_pairs={{0,1},{1,2},{2,3},{3,4},{4,5},{5,6},{6,7},{7,8},{8,9},{9,10},{10,1... | collective-permute-start | bytes 294920 | tf_op jit(solution)/shard_map/ppermute | solution.py:14
  11.7 1.0 reverse_bitcast_fusion.2
  12.7 0.2 copy.32
  12.9 4.2 %reverse_bitcast_fusion.1 = bf16[27,256,256]{1,2,0:T(8,128)(2,1)} fusion(bf16[27,256,256]{2,1,0:T(8,128)(2,1)} %bitcast.59), kind=kLoop, calls=%fused_computation.3 | loop fusion | bytes 7077888 | tf_op jit(solution)/shard_map/transpose | solution.py:30
  17.1 5.7 %copy.29 = bf16[27,256,256]{2,1,0:T(8,128)(2,1)} copy(bf16[27,256,256]{1,2,0:T(8,128)(2,1)} %reverse_bitcast_fusion.1) | data formatting | bytes 7077888 | tf_op jit(solution)/shard_map/transpose | solution.py:30
  22.8 4.2 %reverse_bitcast_fusion = bf16[27,256,256]{1,2,0:T(8,128)(2,1)} fusion(bf16[27,256,256]{2,1,0:T(8,128)(2,1)} %bitcast.60), kind=kLoop, calls=%fused_computation.2 | loop fusion | bytes 7077888 | tf_op jit(solution)/shard_map/transpose | solution.py:30
  27.1 5.8 %copy.34 = bf16[27,256,256]{2,1,0:T(8,128)(2,1)} copy(bf16[27,256,256]{1,2,0:T(8,128)(2,1)} %reverse_bitcast_fusion) | data formatting | bytes 7077888 | tf_op jit(solution)/shard_map/transpose | solution.py:30
  33.1 0.0 copy-start.2
  33.7 1.5 %copy-done.2 = bf16[6912,256]{1,0:T(8,128)(2,1)S(1)} copy-done((bf16[6912,256]{1,0:T(8,128)(2,1)S(1)}, bf16[6912,256]{1,0:T(8,128)(2,1)}, u32[]{:S(2)}) %copy-start.2) | copy-done | bytes 3538968
  35.1 0.9 add_convert_fusion
  36.1 0.1 copy.43
  36.2 0.3 convolution_convert_fusion
  36.5 4.5 %collective-permute-start.3 = (bf16[1,6,4,256]{3,2,1,0:T(4,128)(2,1)S(1)}, bf16[1,6,4,256]{3,2,1,0:T(4,128)(2,1)S(1)}, u32[]{:S(2)}, u32[]{:S(2)}) collective-permute-start(bf16[1,6,4,256]{3,2,1,0:T(4,128)(2,1)S(1)} %reshape.76), channel_id=1, source_target_pairs={{0,1},{1,2},{2,3},{3,4},{4,5},{5,6},{6,7},{7,8},{8,9},{9,10},{10,1... | collective-permute-start | bytes 36872 | tf_op jit(solution)/shard_map/ppermute | solution.py:14
  41.0 4.3 %collective-permute-start.2 = (bf16[1,6,4,256]{3,2,1,0:T(4,128)(2,1)S(1)}, bf16[1,6,4,256]{3,2,1,0:T(4,128)(2,1)S(1)}, u32[]{:S(2)}, u32[]{:S(2)}) collective-permute-start(bf16[1,6,4,256]{3,2,1,0:T(4,128)(2,1)S(1)} %reshape.76), channel_id=1, source_target_pairs={{0,2},{1,3},{2,4},{3,5},{4,6},{5,7},{6,8},{7,9},{8,10},{9,11},{10,... | collective-permute-start | bytes 36872 | tf_op jit(solution)/shard_map/ppermute | solution.py:14
  45.3 0.0 collective-permute-done
  46.1 1.5 %copy-done.3 = bf16[27,256,256]{2,1,0:T(8,128)(2,1)S(1)} copy-done((bf16[27,256,256]{2,1,0:T(8,128)(2,1)S(1)}, bf16[27,256,256]{2,1,0:T(8,128)(2,1)}, u32[]{:S(2)}) %copy-start.3) | copy-done | bytes 3538968
  47.6 0.9 fusion.2
  48.4 0.1 reshape_reshape_reshape.6
  48.5 0.1 copy.44
  48.6 0.7 reshape_reshape.12
  49.3 0.0 all-gather.2.cloned.1.call-update
  49.4 0.0 collective-permute-done.2
  49.4 0.3 divide_convert_fusion
  49.7 1.3 %fusion.6 = bf16[24,256]{1,0:T(8,128)(2,1)S(1)} fusion(bf16[24,2048]{1,0:T(8,128)(2,1)} %reshape_reshape.12, bf16[256,2048]{1,0:T(8,128)(2,1)S(1)} %copy-done.5, f32[24,256]{1,0:T(8,128)S(1)} %get-tuple-element.8, f32[256]{0:T(256)S(1)} %add_multiply_fusion), kind=kOutput, calls=%fused_computation.88 | convolution fusion | flops 25227264 | bytes 1184768 | tf_op jit(solution)/shard_map/dot_general | solution.py:57
  51.0 1.3 %collective-permute-start.5 = (bf16[1,6,4,256]{3,2,1,0:T(4,128)(2,1)S(1)}, bf16[1,6,4,256]{3,2,1,0:T(4,128)(2,1)S(1)}, u32[]{:S(2)}, u32[]{:S(2)}) collective-permute-start(bf16[1,6,4,256]{3,2,1,0:T(4,128)(2,1)S(1)} %reshape.77), channel_id=1, source_target_pairs={{2,0},{3,1},{4,2},{5,3},{6,4},{7,5},{8,6},{9,7},{10,8},{11,9},{12,... | collective-permute-start | bytes 36872 | tf_op jit(solution)/shard_map/ppermute | solution.py:14
  52.3 1.3 %collective-permute-start.4 = (bf16[1,6,4,256]{3,2,1,0:T(4,128)(2,1)S(1)}, bf16[1,6,4,256]{3,2,1,0:T(4,128)(2,1)S(1)}, u32[]{:S(2)}, u32[]{:S(2)}) collective-permute-start(bf16[1,6,4,256]{3,2,1,0:T(4,128)(2,1)S(1)} %reshape.77), channel_id=1, source_target_pairs={{1,0},{2,1},{3,2},{4,3},{5,4},{6,5},{7,6},{8,7},{9,8},{10,9},{11,1... | collective-permute-start | bytes 36872 | tf_op jit(solution)/shard_map/ppermute | solution.py:14
  53.6 0.1 reshape_reshape_reshape.7
  53.8 0.1 reshape_reshape.15
  53.9 0.1 pad_maximum_fusion.1
  54.0 0.6 reshape.83
  54.6 0.7 copy.35
  55.4 7.8 %all-to-all-start = ((bf16[16,24,192]{2,1,0:T(8,128)(2,1)}), bf16[16,24,192]{2,1,0:T(8,128)(2,1)S(1)}, u32[]{:S(2)}, u32[]{:S(2)}) async-start(bf16[16,24,192]{2,1,0:T(8,128)(2,1)} %copy.35), calls=%async_computation | async-start | bytes 393216 | tf_op jit(solution)/shard_map/all_to_all | solution.py:189
  63.2 0.1 convolution_convert_fusion.2
  63.4 0.4 fusion.25
  63.8 0.2 reshape_reshape.14
  64.0 0.1 reshape.80
  64.2 0.1 multiply_convert_fusion
  64.2 1.3 %collective-permute-start.6 = (bf16[2,12,8,256]{3,2,1,0:T(8,128)(2,1)S(1)}, bf16[2,12,8,256]{3,2,1,0:T(8,128)(2,1)S(1)}, u32[]{:S(2)}, u32[]{:S(2)}) collective-permute-start(bf16[2,12,8,256]{3,2,1,0:T(8,128)(2,1)S(1)} %multiply_convert_fusion), channel_id=1, source_target_pairs={{1,0},{2,1},{3,2},{4,3},{5,4},{6,5},{7,6},{8,7},{9,8},{10,9},{11,1... | collective-permute-start | bytes 294920 | tf_op jit(solution)/shard_map/ppermute | solution.py:14
  65.5 24.2 %all_gather.6 = bf16[384,512]{1,0:T(8,128)(2,1)S(1)} all-gather(bf16[24,512]{1,0:T(8,128)(2,1)S(1)} %pad_maximum_fusion.3), channel_id=1, replica_groups=mesh['grp'=2,'tm'=16] {'tm'}, dimensions={0}, use_global_device_ids=true | all-gather | bytes 417792 | tf_op jit(solution)/shard_map/all_gather | solution.py:191
  89.8 0.0 collective-permute-done.6
  90.5 1.5 %copy-done.1 = bf16[27,256,256]{2,1,0:T(8,128)(2,1)S(1)} copy-done((bf16[27,256,256]{2,1,0:T(8,128)(2,1)S(1)}, bf16[27,256,256]{2,1,0:T(8,128)(2,1)}, u32[]{:S(2)}) %copy-start.1) | copy-done | bytes 3538968
  92.0 1.5 %fusion.3 = bf16[2,12,8,256]{3,2,1,0:T(8,128)(2,1)} fusion(f32[2,12,8,256]{3,2,1,0:T(8,128)S(1)} %reshape.80, bf16[2,12,8,6912]{3,2,1,0:T(8,128)(2,1)S(1)} %constant_dynamic-update-slice_fusion.58, bf16[6912,256,1,1]{1,0,3,2:T(8,128)(2,1)S(1)} %bitcast.58), kind=kOutput, calls=%fused_computation.80 | convolution fusion | flops 679575552 | bytes 6488064 | tf_op jit(solution)/shard_map/dot_general | solution.py:84
  93.5 0.8 convolution_multiply_fusion.2
  94.3 0.9 convolution_multiply_fusion.1
  95.2 2.5 %convolution_multiply_fusion = f32[16,2048]{1,0:T(8,128)} fusion(bf16[384,2048]{1,0:T(8,128)(2,1)} %all-gather.2.cloned.1.call-done, bf16[384,192]{1,0:T(8,128)(2,1)S(1)} %bitcast.66), kind=kOutput, calls=%fused_computation.4 | convolution fusion | flops 25198592 | bytes 1802240 | tf_op jit(solution)/shard_map/dot_general | solution.py:51
  (118 shorter events, 2.0 us)
Async XLA Ops:
  7.2 29.1 %copy-start = (bf16[2048,256]{1,0:T(8,128)(2,1)S(1)}, bf16[2048,256]{1,0:T(8,128)(2,1)}, u32[]{:S(2)}) copy-start(bf16[2048,256]{1,0:T(8,128)(2,1)} %param.11) | copy-start | bytes 3145732
  7.2 88.1 %all-gather.2.cloned.1.call-start = ((), (), s32[]{:S(2)}) async-start(), calls=%async_computation.1 | async-start | bytes 1671168 | tf_op jit(solution)/shard_map/all_gather | solution.py:192
  7.2 38.1 %collective-permute-start = (bf16[2,12,8,256]{3,2,1,0:T(8,128)(2,1)}, bf16[2,12,8,256]{3,2,1,0:T(8,128)(2,1)S(1)}, u32[]{:S(2)}, u32[]{:S(2)}) collective-permute-start(bf16[2,12,8,256]{3,2,1,0:T(8,128)(2,1)} %param.9), channel_id=1, source_target_pairs={{1,0},{2,1},{3,2},{4,3},{5,4},{6,5},{7,6},{8,7},{9,8},{10,9},{11,1... | collective-permute-start | bytes 294920 | tf_op jit(solution)/shard_map/ppermute | solution.py:14
  8.7 24.2 %collective-permute-start.1 = (bf16[2,12,8,256]{3,2,1,0:T(8,128)(2,1)}, bf16[2,12,8,256]{3,2,1,0:T(8,128)(2,1)S(1)}, u32[]{:S(2)}, u32[]{:S(2)}) collective-permute-start(bf16[2,12,8,256]{3,2,1,0:T(8,128)(2,1)} %param.8), channel_id=1, source_target_pairs={{0,1},{1,2},{2,3},{3,4},{4,5},{5,6},{6,7},{7,8},{8,9},{9,10},{10,1... | collective-permute-start | bytes 294920 | tf_op jit(solution)/shard_map/ppermute | solution.py:14
  17.1 5.7 %copy-start.8 = (s32[256]{0:T(256)S(1)}, s32[256]{0:T(256)}, u32[]{:S(2)}) copy-start(s32[256]{0:T(256)} %param.15) | copy-start | bytes 3076
  27.1 5.8 %copy-start.7 = (bf16[2,12,8,256]{3,2,1,0:T(8,128)(2,1)S(1)}, bf16[2,12,8,256]{3,2,1,0:T(8,128)(2,1)}, u32[]{:S(2)}) copy-start(bf16[2,12,8,256]{3,2,1,0:T(8,128)(2,1)} %param.9) | copy-start | bytes 294916
  27.1 5.8 %copy-start.6 = (bf16[2,12,8,256]{3,2,1,0:T(8,128)(2,1)S(1)}, bf16[2,12,8,256]{3,2,1,0:T(8,128)(2,1)}, u32[]{:S(2)}) copy-start(bf16[2,12,8,256]{3,2,1,0:T(8,128)(2,1)} %param.8) | copy-start | bytes 294916
  33.1 2.0 %copy-start.2 = (bf16[6912,256]{1,0:T(8,128)(2,1)S(1)}, bf16[6912,256]{1,0:T(8,128)(2,1)}, u32[]{:S(2)}) copy-start(bf16[6912,256]{1,0:T(8,128)(2,1)} %param.10) | copy-start | bytes 10616836
  36.5 12.8 %collective-permute-start.3 = (bf16[1,6,4,256]{3,2,1,0:T(4,128)(2,1)S(1)}, bf16[1,6,4,256]{3,2,1,0:T(4,128)(2,1)S(1)}, u32[]{:S(2)}, u32[]{:S(2)}) collective-permute-start(bf16[1,6,4,256]{3,2,1,0:T(4,128)(2,1)S(1)} %reshape.76), channel_id=1, source_target_pairs={{0,1},{1,2},{2,3},{3,4},{4,5},{5,6},{6,7},{7,8},{8,9},{9,10},{10,1... | collective-permute-start | bytes 36872 | tf_op jit(solution)/shard_map/ppermute | solution.py:14
  41.0 8.3 %collective-permute-start.2 = (bf16[1,6,4,256]{3,2,1,0:T(4,128)(2,1)S(1)}, bf16[1,6,4,256]{3,2,1,0:T(4,128)(2,1)S(1)}, u32[]{:S(2)}, u32[]{:S(2)}) collective-permute-start(bf16[1,6,4,256]{3,2,1,0:T(4,128)(2,1)S(1)} %reshape.76), channel_id=1, source_target_pairs={{0,2},{1,3},{2,4},{3,5},{4,6},{5,7},{6,8},{7,9},{8,10},{9,11},{10,... | collective-permute-start | bytes 36872 | tf_op jit(solution)/shard_map/ppermute | solution.py:14
  45.6 2.0 %copy-start.3 = (bf16[27,256,256]{2,1,0:T(8,128)(2,1)S(1)}, bf16[27,256,256]{2,1,0:T(8,128)(2,1)}, u32[]{:S(2)}) copy-start(bf16[27,256,256]{2,1,0:T(8,128)(2,1)} %copy.29) | copy-start | bytes 10616836
  47.6 1.8 %copy-start.4 = (bf16[768,256]{1,0:T(8,128)(2,1)S(1)}, bf16[768,256]{1,0:T(8,128)(2,1)}, u32[]{:S(2)}) copy-start(bf16[768,256]{1,0:T(8,128)(2,1)} %param.12) | copy-start | bytes 1179652
  47.6 2.1 %copy-start.5 = (bf16[256,2048]{1,0:T(8,128)(2,1)S(1)}, bf16[256,2048]{1,0:T(8,128)(2,1)}, u32[]{:S(2)}) copy-start(bf16[256,2048]{1,0:T(8,128)(2,1)} %param.13) | copy-start | bytes 3145732
  51.0 12.1 %collective-permute-start.5 = (bf16[1,6,4,256]{3,2,1,0:T(4,128)(2,1)S(1)}, bf16[1,6,4,256]{3,2,1,0:T(4,128)(2,1)S(1)}, u32[]{:S(2)}, u32[]{:S(2)}) collective-permute-start(bf16[1,6,4,256]{3,2,1,0:T(4,128)(2,1)S(1)} %reshape.77), channel_id=1, source_target_pairs={{2,0},{3,1},{4,2},{5,3},{6,4},{7,5},{8,6},{9,7},{10,8},{11,9},{12,... | collective-permute-start | bytes 36872 | tf_op jit(solution)/shard_map/ppermute | solution.py:14
  52.3 10.9 %collective-permute-start.4 = (bf16[1,6,4,256]{3,2,1,0:T(4,128)(2,1)S(1)}, bf16[1,6,4,256]{3,2,1,0:T(4,128)(2,1)S(1)}, u32[]{:S(2)}, u32[]{:S(2)}) collective-permute-start(bf16[1,6,4,256]{3,2,1,0:T(4,128)(2,1)S(1)} %reshape.77), channel_id=1, source_target_pairs={{1,0},{2,1},{3,2},{4,3},{5,4},{6,5},{7,6},{8,7},{9,8},{10,9},{11,1... | collective-permute-start | bytes 36872 | tf_op jit(solution)/shard_map/ppermute | solution.py:14
  55.4 38.2 %all-to-all-start = ((bf16[16,24,192]{2,1,0:T(8,128)(2,1)}), bf16[16,24,192]{2,1,0:T(8,128)(2,1)S(1)}, u32[]{:S(2)}, u32[]{:S(2)}) async-start(bf16[16,24,192]{2,1,0:T(8,128)(2,1)} %copy.35), calls=%async_computation | async-start | bytes 393216 | tf_op jit(solution)/shard_map/all_to_all | solution.py:189
  64.2 25.5 %collective-permute-start.6 = (bf16[2,12,8,256]{3,2,1,0:T(8,128)(2,1)S(1)}, bf16[2,12,8,256]{3,2,1,0:T(8,128)(2,1)S(1)}, u32[]{:S(2)}, u32[]{:S(2)}) collective-permute-start(bf16[2,12,8,256]{3,2,1,0:T(8,128)(2,1)S(1)} %multiply_convert_fusion), channel_id=1, source_target_pairs={{1,0},{2,1},{3,2},{4,3},{5,4},{6,5},{7,6},{8,7},{9,8},{10,9},{11,1... | collective-permute-start | bytes 294920 | tf_op jit(solution)/shard_map/ppermute | solution.py:14
  90.0 2.0 %copy-start.1 = (bf16[27,256,256]{2,1,0:T(8,128)(2,1)S(1)}, bf16[27,256,256]{2,1,0:T(8,128)(2,1)}, u32[]{:S(2)}) copy-start(bf16[27,256,256]{2,1,0:T(8,128)(2,1)} %copy.34) | copy-start | bytes 10616836
Sparse Core Ops, SparseCore 0:
  49.5 41.1 all-gather.1
